TPU v7x, 32 devices: a whole 2x2x4 slice. The times are simulated.
32 devices in a mesh: graph: 8 (over z, y), sample: 4 (over x, core).
Axes of the slice: x: 2, y: 2, z: 4, core: 2. Of those that a mesh axis runs over, the one named last changes fastest.
Arguments:
- grid_in: bfloat16 [4, 4096, 256], P('sample', 'graph'), may hold values from -6 to 6
- mesh_init: bfloat16 [4, 1024, 512], P('sample', 'graph'), may hold values from -6 to 6
- g2m_geometry: bfloat16 [4, 8192], P(None, 'graph'), may hold values from -6 to 6
- w_embed: bfloat16 [256, 512], replicated, may hold values from -0.375 to 0.375
- w_g2m: bfloat16 [512, 512], replicated, may hold values from -0.25 to 0.25
- w_geo: bfloat16 [4, 512], replicated, may hold values from -3 to 3
- a_send: bfloat16 [512, 512], replicated, may hold values from -0.25 to 0.25
- a_recv: bfloat16 [512, 512], replicated, may hold values from -0.25 to 0.25
- b_node: bfloat16 [512, 512], replicated, may hold values from -0.25 to 0.25
- cotangent: bfloat16 [4, 1024, 512], P('sample', 'graph'), may hold values from -6 to 6
- g2m_send_rows: int32 [8, 8, 8], P('graph'), may hold values from 0 to 511
- g2m_counts: int32 [8, 8], P('graph'), may hold values from 0 to 8, as said below
- g2m_senders: int32 [8192], P('graph'), may hold values from 0 to 63
- g2m_receivers: int32 [8192], P('graph'), may hold values from 0 to 127
- mesh_send_rows: int32 [8, 8, 4], P('graph'), may hold values from 0 to 127
- mesh_senders: int32 [4096], P('graph'), may hold values from 0 to 159
- mesh_receivers: int32 [4096], P('graph'), may hold values from 0 to 127
Outputs:
- mesh_out: bfloat16 [4, 1024, 512], P('sample', 'graph')
- grad_mesh: float32 [4, 1024, 512], P('sample', 'graph')
- grad_weights: float32 [1536, 512], P('graph')
Inputs may be any that keep to these rules, and one draw needn't show every extreme that they name: `g2m_send_rows`: entry [b, g, j] is a row of band b's own 512 rows. `g2m_counts`: entry [b, g] is the number of live slots from band b to partition g; every band has some partition at 8, and some partition receives 8 from every band. `g2m_senders`: b * 8 + j names slot j from band b, for the partition that holds the edge. `g2m_receivers`: A node of the partition that holds the edge. `mesh_send_rows`: entry [b, g, j] is a row of partition b's own 128 rows. `mesh_senders`: A row of the holding partition's sender_table: below 32 a row received from another partition, else a local node. `mesh_receivers`: A node of the partition that holds the edge.
All inputs are finite; a program needn't handle non-finite values.
Results may differ from a plain program's by a relative error of at most 0.012.
The roundings to bfloat16 on the way count: a program that leaves them out, or rounds other values in their place, can miss the bound.
Values may be sent and summed in bfloat16 or wider, within the bound.
A program may use at most 64 MiB of HBM per device.

v0:
```python
import functools

import jax
import jax.numpy as jnp
from jax import lax
from jax.experimental import pallas as pl
from jax.experimental.pallas import tpu as pltpu
from jax.sharding import PartitionSpec as P

PAD = 8
TILE = 16
BF = jnp.bfloat16
F32 = jnp.float32


def logistic(v):
    return 0.5 + 0.5 * jnp.tanh(0.5 * v)


def dot(left, right):
    return jnp.dot(left, right, preferred_element_type=F32)


def times_transposed(left, right):
    return lax.dot_general(left, right, (((1,), (1,)), ((), ())), preferred_element_type=F32)


def inner_rows(left, right):
    return lax.dot_general(left, right, (((0,), (0,)), ((), ())), preferred_element_type=F32)


def hot(rows, index_row):
    shape = (rows, index_row.shape[1])
    return jnp.where(lax.broadcasted_iota(jnp.int32, shape, 0) == index_row, 1.0, 0.0).astype(BF)


def two_terms(values):
    high = values.astype(BF)
    return jnp.concatenate([high, (values - high.astype(F32)).astype(BF)], axis=0)


def repack(position, count):
    return position if count == PAD else position + lax.div(position, count) * (PAD - count)


def spread(table, pattern):
    low = lax.rem(table, 256)
    return dot(lax.div(table, 256).astype(BF), pattern) * 256.0 + dot(low.astype(BF), pattern)


def slot_rows(grid_rows_ref, counts_ref, halo_rows_ref, groups, padded, halos):
    def grid_of(rows):
        row = lax.broadcasted_iota(jnp.int32, (rows, padded), 0)
        return row, lax.broadcasted_iota(jnp.int32, (rows, padded), 1)

    peer, column = grid_of(groups)
    by_peer = lax.div(column, PAD) == peer
    peer_hot = jnp.where(by_peer, 1.0, 0.0).astype(BF)
    slot, column = grid_of(grid_rows_ref.shape[2])
    slot_hot = jnp.where(lax.rem(column, PAD) == slot, 1.0, 0.0).astype(BF)
    picked = jnp.sum(jnp.where(by_peer, spread(grid_rows_ref[0], slot_hot), 0.0), axis=0, keepdims=True)
    live = dot(counts_ref[...].astype(BF), peer_hot)
    _, column = grid_of(1)
    position = lax.rem(column, PAD)
    grid_rows = jnp.where(position.astype(F32) < live, picked, -1.0).astype(jnp.int32)
    slot, column = grid_of(halos)
    by_slot = lax.rem(column, PAD) == slot
    picked = jnp.sum(jnp.where(by_slot, spread(halo_rows_ref[0], peer_hot), 0.0), axis=0, keepdims=True)
    halo_rows = jnp.where(position < halos, picked, -1.0).astype(jnp.int32)
    return grid_rows, halo_rows


def kernel(
    cfg,
    grid_rows_ref, counts_ref, halo_rows_ref, g2m_senders_ref, g2m_receivers_ref, mesh_senders_ref, mesh_receivers_ref,
    geom_ref, w_geo_ref,
    grid_hbm, init_hbm, w_embed_hbm, w_g2m_hbm, a_send_hbm, a_recv_hbm, b_node_hbm, cot_hbm,
    out_ref, grad_ref, weights_ref,
    grid_v, init_v, w_embed_v, w_g2m_v, a_send_v, a_recv_v, b_node_v, cot_v,
    lat_send, lat_recv, halo_send, halo_recv, back_send, back_recv,
    geo_part, slope_v, local_grad, grads, pair_recv, staged, graph_recv, x_send, x_recv, last_send, last_recv,
    load_sem, g_send_sem, g_recv_sem, pair_sem, tail_sem,
):
    groups, slots, halos, fused = cfg
    me = lax.axis_index("graph")
    sample = lax.axis_index("sample")
    half = lax.rem(sample, 2)
    core_peer = sample + 1 - 2 * half
    far_peer = lax.rem(sample + 2, 4)

    loads = []
    for i, (src, dst) in enumerate(
        [
            (grid_hbm.at[0], grid_v), (w_embed_hbm, w_embed_v), (w_g2m_hbm, w_g2m_v),
            (init_hbm.at[0], init_v), (a_send_hbm, a_send_v), (a_recv_hbm, a_recv_v),
            (b_node_hbm, b_node_v), (cot_hbm.at[0], cot_v),
        ]
    ):
        copy = pltpu.make_async_copy(src, dst, load_sem.at[i])
        if i < 4:
            copy.start()
        loads.append(copy)
    ld_grid, ld_embed, ld_g2m, ld_init, ld_asend, ld_arecv, ld_bnode, ld_cot = loads

    barrier = pltpu.get_barrier_semaphore()

    def greet(step, carry):
        pl.semaphore_signal(barrier, inc=1, device_id={"graph": lax.rem(me + step, groups)}, device_id_type=pl.DeviceIdType.MESH)
        return carry

    lax.fori_loop(1, groups, greet, 0)
    greeted = groups - 1
    if fused:
        for peer in (core_peer, far_peer):
            pl.semaphore_signal(barrier, inc=1, device_id={"sample": peer}, device_id_type=pl.DeviceIdType.MESH)
        greeted += 2

    def swap_copy(kind, src, dst, peer, slot):
        return pltpu.make_async_remote_copy(
            src_ref=src, dst_ref=dst, send_sem=g_send_sem.at[kind, peer], recv_sem=g_recv_sem.at[kind, slot],
            device_id={"graph": peer}, device_id_type=pl.DeviceIdType.MESH,
        )

    def swap_start(kind, source, target):
        def body(step, carry):
            peer = lax.rem(me + step, groups)
            swap_copy(kind, source.at[peer], target.at[me], peer, me).start()
            return carry

        lax.fori_loop(1, groups, body, 0)

    def swap_wait(kind, source, target):
        def body(step, carry):
            peer = lax.rem(me + step, groups)
            swap_copy(kind, source.at[peer], target.at[peer], peer, peer).wait()
            return carry

        lax.fori_loop(1, groups, body, 0)

    width = w_g2m_v.shape[1]
    mesh_rows = init_v.shape[0]
    padded = groups * PAD
    grid_rows, halo_rows = slot_rows(grid_rows_ref, counts_ref, halo_rows_ref, groups, padded, halos)

    pick_grid = hot(grid_v.shape[0], grid_rows)
    ld_grid.wait()
    chosen = inner_rows(pick_grid, grid_v[...]).astype(BF)
    ld_embed.wait()
    for copy in loads[4:]:
        copy.start()
    embedded = dot(chosen, w_embed_v[...])
    lat_send[...] = (embedded * logistic(embedded)).astype(BF).reshape(groups, PAD, width)
    pl.semaphore_wait(barrier, greeted)
    swap_start(0, lat_send, lat_recv)
    lat_recv[me] = lat_send[me]
    geo_part[...] = inner_rows(geom_ref[...], w_geo_ref[...])
    grid_hot = hot(padded, repack(g2m_senders_ref[...], slots))
    recv_hot_g = hot(mesh_rows, g2m_receivers_ref[...])
    ld_g2m.wait()
    ld_init.wait()
    swap_wait(0, lat_send, lat_recv)
    grid_proj = dot(lat_recv[...].reshape(padded, width), w_g2m_v[...])
    grid_proj = two_terms(grid_proj)
    grid_hot = jnp.concatenate([grid_hot, grid_hot], axis=0)
    summed = init_v[...].astype(F32)
    edges = grid_hot.shape[1]
    chunk = 256 if edges % 256 == 0 else edges
    for first in range(0, edges, chunk):
        v = inner_rows(grid_hot[:, first : first + chunk], grid_proj) + geo_part[first : first + chunk, :]
        message = (v * logistic(v)).astype(BF)
        summed = summed + dot(recv_hot_g[:, first : first + chunk], message)
    latent = summed.astype(BF)

    pick_halo = hot(mesh_rows, halo_rows)
    halo_send[...] = inner_rows(pick_halo, latent).astype(BF).reshape(groups, PAD, width)
    swap_start(1, halo_send, halo_recv)
    halo_recv[me] = halo_send[me]
    ld_asend.wait()
    ld_arecv.wait()
    recv_proj = dot(latent, a_recv_v[...])
    local_proj = dot(latent, a_send_v[...])
    recv_hot = hot(mesh_rows, mesh_receivers_ref[...])
    table_row = mesh_senders_ref[...]
    table_row = jnp.where(
        table_row < groups * halos, repack(table_row, halos), table_row + (padded - groups * halos)
    )
    send_hot = hot(padded + mesh_rows, table_row)
    ld_bnode.wait()
    ld_cot.wait()
    swap_wait(1, halo_send, halo_recv)
    halo = halo_recv[...].reshape(padded, width)
    halo_proj = dot(halo, a_send_v[...])
    all_proj = two_terms(jnp.concatenate([halo_proj, local_proj, recv_proj], axis=0))
    all_hot = jnp.concatenate([send_hot, recv_hot], axis=0)
    twice_hot = jnp.concatenate([all_hot, all_hot], axis=0)
    mesh_edges = recv_hot.shape[1]
    chunk = 256 if mesh_edges % 256 == 0 else mesh_edges
    agg = jnp.zeros((mesh_rows, width), F32)
    for first in range(0, mesh_edges, chunk):
        v = inner_rows(twice_hot[:, first : first + chunk], all_proj)
        s = logistic(v)
        slope_v[first : first + chunk, :] = s * (1.0 + v * (1.0 - s))
        agg = agg + dot(recv_hot[:, first : first + chunk], (v * s).astype(BF))
    aggregate = agg.astype(BF)
    update = dot(aggregate, b_node_v[...])
    s = logistic(update)
    out_ref[0] = (latent.astype(F32) + update * s).astype(BF)
    cot = cot_v[...].astype(F32)
    d_update = (cot * (s * (1.0 + update * (1.0 - s)))).astype(BF)
    d_aggregate = times_transposed(d_update, b_node_v[...]).astype(BF)

    kind = BF if fused else F32
    target = grads if fused else weights_ref
    unit = staged.shape[1]
    waiting = list(range(groups))

    def rows_of(block, side):
        return pl.ds(pl.multiple_of((2 * block + side) * unit, TILE), unit)

    def pair_copy(block):
        return pltpu.make_async_remote_copy(
            src_ref=grads.at[rows_of(block, 1 - half)], dst_ref=pair_recv.at[block],
            send_sem=pair_sem.at[0, block], recv_sem=pair_sem.at[1, block],
            device_id={"sample": core_peer}, device_id_type=pl.DeviceIdType.MESH,
        )

    def store_part(number, value):
        target[number * width : (number + 1) * width, :] = value.astype(kind)

    def send_pairs(ready_from):
        while waiting and waiting[-1] * 2 * unit >= ready_from:
            pair_copy(waiting.pop()).start()

    store_part(2, inner_rows(aggregate, d_update))
    if fused:
        send_pairs(2 * width)
    d_both = jnp.zeros((padded + 2 * mesh_rows, width), F32)
    for first in range(0, mesh_edges, chunk):
        d_pre = (inner_rows(recv_hot[:, first : first + chunk], d_aggregate) * slope_v[first : first + chunk, :]).astype(BF)
        d_both = d_both + dot(all_hot[:, first : first + chunk], d_pre)
    d_both = d_both.astype(BF)
    halo_grad = d_both[:padded]
    send_grad = d_both[padded : padded + mesh_rows]
    recv_grad = d_both[padded + mesh_rows :]
    back_send[...] = times_transposed(halo_grad, a_send_v[...]).astype(BF).reshape(groups, PAD, width)
    swap_start(2, back_send, back_recv)
    back_recv[me] = back_send[me]

    def finish_mesh():
        local_grad[...] = cot + times_transposed(recv_grad, a_recv_v[...]) + times_transposed(send_grad, a_send_v[...])
        swap_wait(2, back_send, back_recv)
        grad_ref[0] = local_grad[...] + dot(pick_halo, back_recv[...].reshape(padded, width))

    if not fused:
        store_part(1, inner_rows(latent, recv_grad))
        store_part(0, inner_rows(halo, halo_grad) + inner_rows(latent, send_grad))
        finish_mesh()
        return

    store_part(1, inner_rows(latent, recv_grad))
    send_pairs(width)
    store_part(0, inner_rows(halo, halo_grad) + inner_rows(latent, send_grad))
    send_pairs(0)
    pieces = 2 if unit % (2 * TILE) == 0 else 1
    piece = unit // pieces
    spans = [pl.ds(i * piece, piece) for i in range(pieces)]

    order = [4, 3, 5, 2, 6, 1, 7, 0] if groups == 8 else list(range(1, groups)) + [0]
    blocks = [lax.rem(me + step, groups) for step in order]
    def piece_copy(i, block, slot):
        return swap_copy(3 + i, staged.at[block, spans[i]], graph_recv.at[slot, spans[i]], block, slot)

    for block in range(groups):
        pair_copy(block).wait()
    for i in range(pieces):
        for block, step in zip(blocks, order):
            own_rows = pl.ds(pl.multiple_of((2 * block + half) * unit + i * piece, TILE), piece)
            staged[block, spans[i], :] = (
                grads[own_rows, :].astype(F32) + pair_recv[block, spans[i], :].astype(F32)
            ).astype(BF)
            if step:
                piece_copy(i, block, me).start()
    finish_mesh()

    def tail_copy(i, kind, src, dst, peer):
        return pltpu.make_async_remote_copy(
            src_ref=src.at[spans[i]], dst_ref=dst.at[spans[i]],
            send_sem=tail_sem.at[2 * kind, i], recv_sem=tail_sem.at[2 * kind + 1, i],
            device_id={"sample": peer}, device_id_type=pl.DeviceIdType.MESH,
        )

    for i in range(pieces):
        total = staged[me, spans[i], :].astype(F32)
        for block, step in zip(blocks, order):
            if step:
                piece_copy(i, block, block).wait()
                total = total + graph_recv[block, spans[i], :].astype(F32)
        x_send[spans[i], :] = total.astype(BF)
        tail_copy(i, 0, x_send, x_recv, far_peer).start()
    for i in range(pieces):
        tail_copy(i, 0, x_send, x_recv, far_peer).wait()
        total = x_send[spans[i], :].astype(F32) + x_recv[spans[i], :].astype(F32)
        last_send[spans[i], :] = total
        tail_copy(i, 1, last_send, last_recv, core_peer).start()
        weights_ref[pl.ds(pl.multiple_of(half * unit + i * piece, 8), piece), :] = total
    for i in range(pieces):
        tail_copy(i, 1, last_send, last_recv, core_peer).wait()
    weights_ref[pl.ds(pl.multiple_of((1 - half) * unit, 8), unit), :] = last_recv[...]


def hand_over(*refs):
    sources, targets, held, sem = refs[:3], refs[3:6], refs[6:9], refs[9]
    inward = [pltpu.make_async_copy(sources[i], held[i], sem.at[i]) for i in range(3)]
    outward = [pltpu.make_async_copy(held[i], targets[i], sem.at[3 + i]) for i in range(3)]
    for copy in inward:
        copy.start()
    for i in range(3):
        inward[i].wait()
        outward[i].start()
    for copy in outward:
        copy.wait()


def on_device(
    grid_in, mesh_init, g2m_geometry, w_embed, w_g2m, w_geo, a_send, a_recv, b_node, cotangent,
    g2m_send_rows, g2m_counts, g2m_senders, g2m_receivers, mesh_send_rows, mesh_senders, mesh_receivers,
):
    groups = lax.axis_size("graph")
    samples = lax.axis_size("sample")
    slots = g2m_send_rows.shape[2]
    halos = mesh_send_rows.shape[2]
    width = w_g2m.shape[1]
    mesh_rows = mesh_init.shape[1]
    block_rows = 3 * width // groups
    fused = samples == 4 and block_rows % (2 * TILE) == 0
    unit = block_rows // 2 if fused else TILE
    weights_shape = (block_rows, width) if fused else (3 * width, width)
    edges, mesh_edges = g2m_senders.shape[0], mesh_senders.shape[0]
    one = groups if fused else 1
    vmem = pl.BlockSpec(memory_space=pltpu.VMEM)
    hbm = pl.BlockSpec(memory_space=pl.ANY)
    slab = pltpu.VMEM((groups, PAD, width), BF)
    mesh_out, grad_mesh, weights = pl.pallas_call(
        functools.partial(kernel, (groups, slots, halos, fused)),
        out_shape=(
            jax.ShapeDtypeStruct(mesh_init.shape, BF),
            jax.ShapeDtypeStruct(mesh_init.shape, F32),
            jax.ShapeDtypeStruct(weights_shape, F32),
        ),
        in_specs=[vmem] * 9 + [hbm] * 8,
        out_specs=(vmem, vmem, vmem),
        scratch_shapes=[
            pltpu.VMEM(grid_in.shape[1:], BF), pltpu.VMEM(mesh_init.shape[1:], BF),
            pltpu.VMEM(w_embed.shape, BF), pltpu.VMEM(w_g2m.shape, BF), pltpu.VMEM(a_send.shape, BF),
            pltpu.VMEM(a_recv.shape, BF), pltpu.VMEM(b_node.shape, BF), pltpu.VMEM(cotangent.shape[1:], BF),
            slab, slab, slab, slab, slab, slab,
            pltpu.VMEM((edges, width), F32), pltpu.VMEM((mesh_edges, width), F32),
            pltpu.VMEM((mesh_rows, width), F32),
            pltpu.VMEM((3 * width, width) if fused else (TILE, width), BF),
            pltpu.VMEM((one, unit, width), BF), pltpu.VMEM((one, unit, width), BF), pltpu.VMEM((one, unit, width), BF),
            pltpu.VMEM((unit, width), BF), pltpu.VMEM((unit, width), BF),
            pltpu.VMEM((unit, width), F32), pltpu.VMEM((unit, width), F32),
            pltpu.SemaphoreType.DMA((8,)), pltpu.SemaphoreType.DMA((5, groups)), pltpu.SemaphoreType.DMA((5, groups)),
            pltpu.SemaphoreType.DMA((2, groups)), pltpu.SemaphoreType.DMA((4, 2)),
        ],
        compiler_params=pltpu.CompilerParams(
            collective_id=0, has_side_effects=True, vmem_limit_bytes=60 * 1024 * 1024
        ),
    )(
        g2m_send_rows, g2m_counts, jnp.swapaxes(mesh_send_rows, 1, 2), g2m_senders[None], g2m_receivers[None],
        mesh_senders[None], mesh_receivers[None], g2m_geometry, w_geo, grid_in, mesh_init, w_embed, w_g2m, a_send, a_recv, b_node, cotangent,
    )
    if not fused:
        weights = lax.psum(lax.psum_scatter(weights, "graph", scatter_dimension=0, tiled=True), "sample")
        return mesh_out, grad_mesh, weights
    results = (mesh_out, grad_mesh, weights)
    return pl.pallas_call(
        hand_over,
        out_shape=tuple(jax.ShapeDtypeStruct(value.shape, value.dtype) for value in results),
        in_specs=[hbm] * 3,
        out_specs=(hbm,) * 3,
        scratch_shapes=[pltpu.VMEM(value.shape, value.dtype) for value in results] + [pltpu.SemaphoreType.DMA((6,))],
    )(*results)


def solution(mesh):
    rows = P("sample", "graph", None)
    placed = (
        rows, rows, P(None, "graph"), P(), P(), P(), P(), P(), P(), rows,
        P("graph", None, None), P("graph", None), P("graph"), P("graph"), P("graph", None, None), P("graph"), P("graph"),
    )
    return jax.shard_map(
        on_device, mesh=mesh, in_specs=placed, out_specs=(rows, rows, P("graph", None)), check_vma=False
    )
```

profile of v0, /device:TPU:17, one launch (start us, length us, event | category | flops | bytes accessed | tf_op | source)
XLA Modules:
  0.0 47.0 jit_solution(16452460694847543285)
XLA Ops:
  0.6 44.4 %shard_map.184 = (bf16[1,128,512]{2,1,0:T(8,128)(2,1)}, f32[1,128,512]{2,1,0:T(8,128)}, f32[192,512]{1,0:T(8,128)}) custom-call(s32[1,8,8]{2,1,0:T(8,128)} %grid_rows_ref.1, s32[1,8]{1,0:T(1,128)} %counts_ref.1, s32[1,4,8]{2,1,0:T(4,128)} %bitcast.7, s32[1,1024]{1,0:T(1,128)} %bitcast.5, s32[1,1024]{1,0:T(1,128)} %bitcast.6, s32[1,512]{1,0:T(1,128)} %bitcast.8, ...), custom_call_target="tpu_custom_call" | custom-call | tf_op jit(solution)/shard_map/pallas_call | solution.py:343
  45.0 1.9 %shard_map.185 = (bf16[1,128,512]{2,1,0:T(8,128)(2,1)}, f32[1,128,512]{2,1,0:T(8,128)}, f32[192,512]{1,0:T(8,128)}) custom-call(bf16[1,128,512]{2,1,0:T(8,128)(2,1)} %get-tuple-element.6.refs_0_, f32[1,128,512]{2,1,0:T(8,128)} %get-tuple-element.7.refs_1_, f32[192,512]{1,0:T(8,128)} %get-tuple-element.8.refs_2_), custom_call_target="tpu_custom_call" | custom-call | tf_op jit(solution)/shard_map/pallas_call | solution.py:377
where the time goes:
time: 47.7 us; the launch traced here: 47 us
  Pallas kernels  46.3 us (97%)
  between operations  0.65 us (1%)
    pallas_call x1, Pallas kernels, on_device(): pl.pallas_call(functools.partial(kernel, (groups, slots, halos, fused)),...  44.4 us
    pallas_call x1, Pallas kernels, on_device(): pl.pallas_call(hand_over, out_shape=tuple((jax.ShapeDtypeStruct(value.sha...  1.95 us

commit v1 on v0

--- a/solution.py
+++ b/solution.py
@@ -9,6 +9,7 @@
 
 PAD = 8
 TILE = 16
+COLUMNS = 2
 BF = jnp.bfloat16
 F32 = jnp.float32
 
@@ -78,15 +79,20 @@
     out_ref, grad_ref, weights_ref,
     grid_v, init_v, w_embed_v, w_g2m_v, a_send_v, a_recv_v, b_node_v, cot_v,
     lat_send, lat_recv, halo_send, halo_recv, back_send, back_recv,
-    geo_part, slope_v, local_grad, grads, pair_recv, staged, graph_recv, x_send, x_recv, last_send, last_recv,
-    load_sem, g_send_sem, g_recv_sem, pair_sem, tail_sem,
+    geo_part, slope_v, local_grad, grads, pair_recv, staged, plane_recv, line_send, line_recv, last_send, last_recv,
+    load_sem, g_send_sem, g_recv_sem, pair_sem, plane_sem, line_sem, last_sem,
 ):
     groups, slots, halos, fused = cfg
     me = lax.axis_index("graph")
     sample = lax.axis_index("sample")
     half = lax.rem(sample, 2)
+    far = lax.div(sample, 2)
+    column = lax.rem(me, COLUMNS)
+    line = lax.div(me, COLUMNS)
     core_peer = sample + 1 - 2 * half
-    far_peer = lax.rem(sample + 2, 4)
+
+    def sample_at(dx, dc):
+        return 2 * lax.rem(far + dx, 2) + lax.rem(half + dc, 2)
 
     loads = []
     for i, (src, dst) in enumerate(
@@ -111,9 +117,12 @@
     lax.fori_loop(1, groups, greet, 0)
     greeted = groups - 1
     if fused:
-        for peer in (core_peer, far_peer):
-            pl.semaphore_signal(barrier, inc=1, device_id={"sample": peer}, device_id_type=pl.DeviceIdType.MESH)
-        greeted += 2
+        other_column = COLUMNS * line + lax.rem(column + 1, COLUMNS)
+        for graph, peer in ((me, core_peer), (me, sample_at(1, 0)), (me, sample_at(1, 1)), (other_column, sample_at(1, 0))):
+            pl.semaphore_signal(
+                barrier, inc=1, device_id={"graph": graph, "sample": peer}, device_id_type=pl.DeviceIdType.MESH
+            )
+        greeted += 4
 
     def swap_copy(kind, src, dst, peer, slot):
         return pltpu.make_async_remote_copy(
@@ -231,6 +240,41 @@
         while waiting and waiting[-1] * 2 * unit >= ready_from:
             pair_copy(waiting.pop()).start()
 
+    quarter = unit // 2
+    lines = groups // COLUMNS
+    steps = [(1, 0), (0, 1), (1, 1)]
+
+    def plane_copy(row, k):
+        dx, dy = steps[k]
+        x, y = lax.rem(far + dx, 2), lax.rem(column + dy, COLUMNS)
+        return pltpu.make_async_remote_copy(
+            src_ref=staged.at[COLUMNS * row + y, pl.ds(pl.multiple_of(x * quarter, TILE), quarter)],
+            dst_ref=plane_recv.at[row, k],
+            send_sem=plane_sem.at[0, row, k], recv_sem=plane_sem.at[1, row, k],
+            device_id={"graph": COLUMNS * line + y, "sample": 2 * x + half}, device_id_type=pl.DeviceIdType.MESH,
+        )
+
+    def line_copy(row, slot):
+        return pltpu.make_async_remote_copy(
+            src_ref=line_send.at[row], dst_ref=line_recv.at[slot],
+            send_sem=line_sem.at[0, row], recv_sem=line_sem.at[1, slot],
+            device_id={"graph": COLUMNS * row + column}, device_id_type=pl.DeviceIdType.MESH,
+        )
+
+    def last_copy(k):
+        return pltpu.make_async_remote_copy(
+            src_ref=last_send, dst_ref=last_recv.at[k],
+            send_sem=last_sem.at[0, k], recv_sem=last_sem.at[1, k],
+            device_id={"sample": sample_at(*steps[k])}, device_id_type=pl.DeviceIdType.MESH,
+        )
+
+    def stage_row(row):
+        for block in range(COLUMNS * row, COLUMNS * (row + 1)):
+            pair_copy(block).wait()
+            staged[block] = (grads[rows_of(block, half), :].astype(F32) + pair_recv[block].astype(F32)).astype(BF)
+        for k in (2, 0, 1):
+            plane_copy(row, k).start()
+
     store_part(2, inner_rows(aggregate, d_update))
     if fused:
         send_pairs(2 * width)
@@ -245,6 +289,8 @@
     back_send[...] = times_transposed(halo_grad, a_send_v[...]).astype(BF).reshape(groups, PAD, width)
     swap_start(2, back_send, back_recv)
     back_recv[me] = back_send[me]
+    if fused:
+        stage_row(lines - 1)
 
     def finish_mesh():
         local_grad[...] = cot + times_transposed(recv_grad, a_recv_v[...]) + times_transposed(send_grad, a_send_v[...])
@@ -261,51 +307,41 @@
     send_pairs(width)
     store_part(0, inner_rows(halo, halo_grad) + inner_rows(latent, send_grad))
     send_pairs(0)
-    pieces = 2 if unit % (2 * TILE) == 0 else 1
-    piece = unit // pieces
-    spans = [pl.ds(i * piece, piece) for i in range(pieces)]
-
-    order = [4, 3, 5, 2, 6, 1, 7, 0] if groups == 8 else list(range(1, groups)) + [0]
-    blocks = [lax.rem(me + step, groups) for step in order]
-    def piece_copy(i, block, slot):
-        return swap_copy(3 + i, staged.at[block, spans[i]], graph_recv.at[slot, spans[i]], block, slot)
-
-    for block in range(groups):
-        pair_copy(block).wait()
-    for i in range(pieces):
-        for block, step in zip(blocks, order):
-            own_rows = pl.ds(pl.multiple_of((2 * block + half) * unit + i * piece, TILE), piece)
-            staged[block, spans[i], :] = (
-                grads[own_rows, :].astype(F32) + pair_recv[block, spans[i], :].astype(F32)
-            ).astype(BF)
-            if step:
-                piece_copy(i, block, me).start()
+    order = [lines - 1, lines - 2] + list(range(lines - 2))
+    for row in order[1:]:
+        stage_row(row)
     finish_mesh()
 
-    def tail_copy(i, kind, src, dst, peer):
-        return pltpu.make_async_remote_copy(
-            src_ref=src.at[spans[i]], dst_ref=dst.at[spans[i]],
-            send_sem=tail_sem.at[2 * kind, i], recv_sem=tail_sem.at[2 * kind + 1, i],
-            device_id={"sample": peer}, device_id_type=pl.DeviceIdType.MESH,
-        )
-
-    for i in range(pieces):
-        total = staged[me, spans[i], :].astype(F32)
-        for block, step in zip(blocks, order):
-            if step:
-                piece_copy(i, block, block).wait()
-                total = total + graph_recv[block, spans[i], :].astype(F32)
-        x_send[spans[i], :] = total.astype(BF)
-        tail_copy(i, 0, x_send, x_recv, far_peer).start()
-    for i in range(pieces):
-        tail_copy(i, 0, x_send, x_recv, far_peer).wait()
-        total = x_send[spans[i], :].astype(F32) + x_recv[spans[i], :].astype(F32)
-        last_send[spans[i], :] = total
-        tail_copy(i, 1, last_send, last_recv, core_peer).start()
-        weights_ref[pl.ds(pl.multiple_of(half * unit + i * piece, 8), piece), :] = total
-    for i in range(pieces):
-        tail_copy(i, 1, last_send, last_recv, core_peer).wait()
-    weights_ref[pl.ds(pl.multiple_of((1 - half) * unit, 8), unit), :] = last_recv[...]
+    own_rows = pl.ds(pl.multiple_of(far * quarter, TILE), quarter)
+    for row in order:
+        total = staged[COLUMNS * row + column, own_rows, :].astype(F32)
+        for k in range(3):
+            plane_copy(row, k).wait()
+            total = total + plane_recv[row, k].astype(F32)
+        line_send[row] = total.astype(BF)
+
+        @pl.when(line != row)
+        def _():
+            line_copy(row, line).start()
+
+    total = line_send[line].astype(F32)
+    for step in range(1, lines):
+        row = lax.rem(line + step, lines)
+        line_copy(row, row).wait()
+        total = total + line_recv[row].astype(F32)
+    last_send[...] = total.astype(BF)
+    for k in (2, 0, 1):
+        last_copy(k).start()
+
+    def place(k, value):
+        dx, dc = steps[k] if k >= 0 else (0, 0)
+        start = lax.rem(half + dc, 2) * unit + lax.rem(far + dx, 2) * quarter
+        weights_ref[pl.ds(pl.multiple_of(start, TILE), quarter), :] = value
+
+    place(-1, total)
+    for k in (1, 0, 2):
+        last_copy(k).wait()
+        place(k, last_recv[k].astype(F32))
 
 
 def hand_over(*refs):
@@ -332,11 +368,13 @@
     width = w_g2m.shape[1]
     mesh_rows = mesh_init.shape[1]
     block_rows = 3 * width // groups
-    fused = samples == 4 and block_rows % (2 * TILE) == 0
+    fused = samples == 4 and groups % COLUMNS == 0 and groups > 2 * COLUMNS and block_rows % (4 * TILE) == 0
     unit = block_rows // 2 if fused else TILE
     weights_shape = (block_rows, width) if fused else (3 * width, width)
     edges, mesh_edges = g2m_senders.shape[0], mesh_senders.shape[0]
     one = groups if fused else 1
+    quarter = unit // 2 if fused else TILE
+    lines = groups // COLUMNS if fused else 1
     vmem = pl.BlockSpec(memory_space=pltpu.VMEM)
     hbm = pl.BlockSpec(memory_space=pl.ANY)
     slab = pltpu.VMEM((groups, PAD, width), BF)
@@ -357,11 +395,12 @@
             pltpu.VMEM((edges, width), F32), pltpu.VMEM((mesh_edges, width), F32),
             pltpu.VMEM((mesh_rows, width), F32),
             pltpu.VMEM((3 * width, width) if fused else (TILE, width), BF),
-            pltpu.VMEM((one, unit, width), BF), pltpu.VMEM((one, unit, width), BF), pltpu.VMEM((one, unit, width), BF),
-            pltpu.VMEM((unit, width), BF), pltpu.VMEM((unit, width), BF),
-            pltpu.VMEM((unit, width), F32), pltpu.VMEM((unit, width), F32),
-            pltpu.SemaphoreType.DMA((8,)), pltpu.SemaphoreType.DMA((5, groups)), pltpu.SemaphoreType.DMA((5, groups)),
-            pltpu.SemaphoreType.DMA((2, groups)), pltpu.SemaphoreType.DMA((4, 2)),
+            pltpu.VMEM((one, unit, width), BF), pltpu.VMEM((one, unit, width), BF),
+            pltpu.VMEM((lines, 3, quarter, width), BF), pltpu.VMEM((lines, quarter, width), BF),
+            pltpu.VMEM((lines, quarter, width), BF), pltpu.VMEM((quarter, width), BF), pltpu.VMEM((3, quarter, width), BF),
+            pltpu.SemaphoreType.DMA((8,)), pltpu.SemaphoreType.DMA((3, groups)), pltpu.SemaphoreType.DMA((3, groups)),
+            pltpu.SemaphoreType.DMA((2, groups)), pltpu.SemaphoreType.DMA((2, lines, 3)),
+            pltpu.SemaphoreType.DMA((2, lines)), pltpu.SemaphoreType.DMA((2, 3)),
         ],
         compiler_params=pltpu.CompilerParams(
             collective_id=0, has_side_effects=True, vmem_limit_bytes=60 * 1024 * 1024

time: 47.7 us -> 43.1 us (0.904)
  the two profiles are of different devices: /device:TPU:17 before, /device:TPU:0 now
where the time goes in v1:
time: 43.1 us; the launch traced here: 42.9 us
  Pallas kernels  42.2 us (98%)
  between operations  0.65 us (2%)
    pallas_call x1, Pallas kernels, on_device(): pl.pallas_call(functools.partial(kernel, (groups, slots, halos, fused)),...  40.3 us
    pallas_call x1, Pallas kernels, on_device(): pl.pallas_call(hand_over, out_shape=tuple((jax.ShapeDtypeStruct(value.sha...  1.95 us

profile of v1, /device:TPU:0, one launch (start us, length us, event | category | flops | bytes accessed | tf_op | source)
XLA Modules:
  0.0 42.9 jit_solution(15251949646213582770)
XLA Ops:
  0.6 40.3 %shard_map.184 = (bf16[1,128,512]{2,1,0:T(8,128)(2,1)}, f32[1,128,512]{2,1,0:T(8,128)}, f32[192,512]{1,0:T(8,128)}) custom-call(s32[1,8,8]{2,1,0:T(8,128)} %grid_rows_ref.1, s32[1,8]{1,0:T(1,128)} %counts_ref.1, s32[1,4,8]{2,1,0:T(4,128)} %bitcast.7, s32[1,1024]{1,0:T(1,128)} %bitcast.5, s32[1,1024]{1,0:T(1,128)} %bitcast.6, s32[1,512]{1,0:T(1,128)} %bitcast.8, ...), custom_call_target="tpu_custom_call" | custom-call | tf_op jit(solution)/shard_map/pallas_call | solution.py:381
  40.9 1.9 %shard_map.185 = (bf16[1,128,512]{2,1,0:T(8,128)(2,1)}, f32[1,128,512]{2,1,0:T(8,128)}, f32[192,512]{1,0:T(8,128)}) custom-call(bf16[1,128,512]{2,1,0:T(8,128)(2,1)} %get-tuple-element.6.refs_0_, f32[1,128,512]{2,1,0:T(8,128)} %get-tuple-element.7.refs_1_, f32[192,512]{1,0:T(8,128)} %get-tuple-element.8.refs_2_), custom_call_target="tpu_custom_call" | custom-call | tf_op jit(solution)/shard_map/pallas_call | solution.py:416

commit v2 on v1

--- a/solution.py
+++ b/solution.py
@@ -9,6 +9,7 @@
 
 PAD = 8
 TILE = 16
+LIMIT = 67043328 - 1024 * 1024
 COLUMNS = 2
 BF = jnp.bfloat16
 F32 = jnp.float32
@@ -73,14 +74,16 @@
 
 def kernel(
     cfg,
+    grid_rows_hbm, counts_hbm, halo_rows_hbm, g2m_senders_hbm, g2m_receivers_hbm, mesh_senders_hbm, mesh_receivers_hbm,
+    geom_hbm, w_geo_hbm,
+    grid_hbm, init_hbm, w_embed_hbm, w_g2m_hbm, a_send_hbm, a_recv_hbm, b_node_hbm, cot_hbm,
+    out_ref, grad_ref, weights_ref,
     grid_rows_ref, counts_ref, halo_rows_ref, g2m_senders_ref, g2m_receivers_ref, mesh_senders_ref, mesh_receivers_ref,
     geom_ref, w_geo_ref,
-    grid_hbm, init_hbm, w_embed_hbm, w_g2m_hbm, a_send_hbm, a_recv_hbm, b_node_hbm, cot_hbm,
-    out_ref, grad_ref, weights_ref,
     grid_v, init_v, w_embed_v, w_g2m_v, a_send_v, a_recv_v, b_node_v, cot_v,
     lat_send, lat_recv, halo_send, halo_recv, back_send, back_recv,
     geo_part, slope_v, local_grad, grads, pair_recv, staged, plane_recv, line_send, line_recv, last_send, last_recv,
-    load_sem, g_send_sem, g_recv_sem, pair_sem, plane_sem, line_sem, last_sem,
+    load_sem, small_sem, g_send_sem, g_recv_sem, pair_sem, plane_sem, line_sem, last_sem,
 ):
     groups, slots, halos, fused = cfg
     me = lax.axis_index("graph")
@@ -94,6 +97,19 @@
     def sample_at(dx, dc):
         return 2 * lax.rem(far + dx, 2) + lax.rem(half + dc, 2)
 
+    small = [
+        pltpu.make_async_copy(src, dst, small_sem.at[i])
+        for i, (src, dst) in enumerate(
+            [
+                (grid_rows_hbm, grid_rows_ref), (counts_hbm, counts_ref), (halo_rows_hbm, halo_rows_ref),
+                (g2m_senders_hbm, g2m_senders_ref), (g2m_receivers_hbm, g2m_receivers_ref),
+                (mesh_senders_hbm, mesh_senders_ref), (mesh_receivers_hbm, mesh_receivers_ref),
+                (geom_hbm, geom_ref), (w_geo_hbm, w_geo_ref),
+            ]
+        )
+    ]
+    for copy in small[:3]:
+        copy.start()
     loads = []
     for i, (src, dst) in enumerate(
         [
@@ -103,7 +119,7 @@
         ]
     ):
         copy = pltpu.make_async_copy(src, dst, load_sem.at[i])
-        if i < 4:
+        if i < 2:
             copy.start()
         loads.append(copy)
     ld_grid, ld_embed, ld_g2m, ld_init, ld_asend, ld_arecv, ld_bnode, ld_cot = loads
@@ -149,6 +165,10 @@
     width = w_g2m_v.shape[1]
     mesh_rows = init_v.shape[0]
     padded = groups * PAD
+    for copy in small[:3]:
+        copy.wait()
+    for copy in small[3:] + loads[2:4]:
+        copy.start()
     grid_rows, halo_rows = slot_rows(grid_rows_ref, counts_ref, halo_rows_ref, groups, padded, halos)
 
     pick_grid = hot(grid_v.shape[0], grid_rows)
@@ -162,6 +182,8 @@
     pl.semaphore_wait(barrier, greeted)
     swap_start(0, lat_send, lat_recv)
     lat_recv[me] = lat_send[me]
+    for copy in small[3:]:
+        copy.wait()
     geo_part[...] = inner_rows(geom_ref[...], w_geo_ref[...])
     grid_hot = hot(padded, repack(g2m_senders_ref[...], slots))
     recv_hot_g = hot(mesh_rows, g2m_receivers_ref[...])
@@ -307,12 +329,23 @@
     send_pairs(width)
     store_part(0, inner_rows(halo, halo_grad) + inner_rows(latent, send_grad))
     send_pairs(0)
-    order = [lines - 1, lines - 2] + list(range(lines - 2))
+    order = [lines - 1] + list(range(lines - 1))
     for row in order[1:]:
         stage_row(row)
     finish_mesh()
 
     own_rows = pl.ds(pl.multiple_of(far * quarter, TILE), quarter)
+
+    def finish_row():
+        total = line_send[line].astype(F32)
+        for step in range(1, lines):
+            row = lax.rem(line + step, lines)
+            line_copy(row, row).wait_recv()
+            total = total + line_recv[row].astype(F32)
+        last_send[...] = total.astype(BF)
+        for k in (2, 0, 1):
+            last_copy(k).start()
+
     for row in order:
         total = staged[COLUMNS * row + column, own_rows, :].astype(F32)
         for k in range(3):
@@ -324,36 +357,31 @@
         def _():
             line_copy(row, line).start()
 
-    total = line_send[line].astype(F32)
-    for step in range(1, lines):
-        row = lax.rem(line + step, lines)
-        line_copy(row, row).wait()
-        total = total + line_recv[row].astype(F32)
-    last_send[...] = total.astype(BF)
-    for k in (2, 0, 1):
-        last_copy(k).start()
+        if row == lines - 2:
+            pl.when(line != 0)(finish_row)
+        if row == lines - 3:
+            pl.when(line == 0)(finish_row)
 
     def place(k, value):
         dx, dc = steps[k] if k >= 0 else (0, 0)
         start = lax.rem(half + dc, 2) * unit + lax.rem(far + dx, 2) * quarter
         weights_ref[pl.ds(pl.multiple_of(start, TILE), quarter), :] = value
 
-    place(-1, total)
+    place(-1, last_send[...].astype(F32))
+    for step in range(1, lines):
+        row = lax.rem(line + step, lines)
+        line_copy(row, row).wait_send()
     for k in (1, 0, 2):
         last_copy(k).wait()
         place(k, last_recv[k].astype(F32))
 
 
 def hand_over(*refs):
-    sources, targets, held, sem = refs[:3], refs[3:6], refs[6:9], refs[9]
-    inward = [pltpu.make_async_copy(sources[i], held[i], sem.at[i]) for i in range(3)]
-    outward = [pltpu.make_async_copy(held[i], targets[i], sem.at[3 + i]) for i in range(3)]
-    for copy in inward:
+    sources, targets, sem = refs[:3], refs[3:6], refs[6]
+    copies = [pltpu.make_async_copy(sources[i], targets[i], sem.at[i]) for i in range(3)]
+    for copy in copies:
         copy.start()
-    for i in range(3):
-        inward[i].wait()
-        outward[i].start()
-    for copy in outward:
+    for copy in copies:
         copy.wait()
 
 
@@ -376,18 +404,20 @@
     quarter = unit // 2 if fused else TILE
     lines = groups // COLUMNS if fused else 1
     vmem = pl.BlockSpec(memory_space=pltpu.VMEM)
-    hbm = pl.BlockSpec(memory_space=pl.ANY)
+    hbm = pl.BlockSpec(memory_space=pltpu.HBM)
     slab = pltpu.VMEM((groups, PAD, width), BF)
+    held = pltpu.VMEM if fused else jax.ShapeDtypeStruct
+    small = (
+        g2m_send_rows, g2m_counts, jnp.swapaxes(mesh_send_rows, 1, 2), g2m_senders[None], g2m_receivers[None],
+        mesh_senders[None], mesh_receivers[None], g2m_geometry, w_geo,
+    )
     mesh_out, grad_mesh, weights = pl.pallas_call(
         functools.partial(kernel, (groups, slots, halos, fused)),
-        out_shape=(
-            jax.ShapeDtypeStruct(mesh_init.shape, BF),
-            jax.ShapeDtypeStruct(mesh_init.shape, F32),
-            jax.ShapeDtypeStruct(weights_shape, F32),
-        ),
-        in_specs=[vmem] * 9 + [hbm] * 8,
+        out_shape=(held(mesh_init.shape, BF), held(mesh_init.shape, F32), held(weights_shape, F32)),
+        in_specs=[hbm] * 17,
         out_specs=(vmem, vmem, vmem),
-        scratch_shapes=[
+        scratch_shapes=[pltpu.VMEM(value.shape, value.dtype) for value in small]
+        + [
             pltpu.VMEM(grid_in.shape[1:], BF), pltpu.VMEM(mesh_init.shape[1:], BF),
             pltpu.VMEM(w_embed.shape, BF), pltpu.VMEM(w_g2m.shape, BF), pltpu.VMEM(a_send.shape, BF),
             pltpu.VMEM(a_recv.shape, BF), pltpu.VMEM(b_node.shape, BF), pltpu.VMEM(cotangent.shape[1:], BF),
@@ -398,27 +428,26 @@
             pltpu.VMEM((one, unit, width), BF), pltpu.VMEM((one, unit, width), BF),
             pltpu.VMEM((lines, 3, quarter, width), BF), pltpu.VMEM((lines, quarter, width), BF),
             pltpu.VMEM((lines, quarter, width), BF), pltpu.VMEM((quarter, width), BF), pltpu.VMEM((3, quarter, width), BF),
-            pltpu.SemaphoreType.DMA((8,)), pltpu.SemaphoreType.DMA((3, groups)), pltpu.SemaphoreType.DMA((3, groups)),
+            pltpu.SemaphoreType.DMA((8,)), pltpu.SemaphoreType.DMA((9,)), pltpu.SemaphoreType.DMA((3, groups)), pltpu.SemaphoreType.DMA((3, groups)),
             pltpu.SemaphoreType.DMA((2, groups)), pltpu.SemaphoreType.DMA((2, lines, 3)),
             pltpu.SemaphoreType.DMA((2, lines)), pltpu.SemaphoreType.DMA((2, 3)),
         ],
         compiler_params=pltpu.CompilerParams(
-            collective_id=0, has_side_effects=True, vmem_limit_bytes=60 * 1024 * 1024
+            collective_id=0, has_side_effects=True, vmem_limit_bytes=LIMIT
         ),
     )(
-        g2m_send_rows, g2m_counts, jnp.swapaxes(mesh_send_rows, 1, 2), g2m_senders[None], g2m_receivers[None],
-        mesh_senders[None], mesh_receivers[None], g2m_geometry, w_geo, grid_in, mesh_init, w_embed, w_g2m, a_send, a_recv, b_node, cotangent,
+        *small, grid_in, mesh_init, w_embed, w_g2m, a_send, a_recv, b_node, cotangent,
     )
     if not fused:
         weights = lax.psum(lax.psum_scatter(weights, "graph", scatter_dimension=0, tiled=True), "sample")
         return mesh_out, grad_mesh, weights
-    results = (mesh_out, grad_mesh, weights)
+    results = tuple(pltpu.with_memory_space_constraint(value, pltpu.VMEM) for value in (mesh_out, grad_mesh, weights))
     return pl.pallas_call(
         hand_over,
         out_shape=tuple(jax.ShapeDtypeStruct(value.shape, value.dtype) for value in results),
-        in_specs=[hbm] * 3,
+        in_specs=[vmem] * 3,
         out_specs=(hbm,) * 3,
-        scratch_shapes=[pltpu.VMEM(value.shape, value.dtype) for value in results] + [pltpu.SemaphoreType.DMA((6,))],
+        scratch_shapes=[pltpu.SemaphoreType.DMA((3,))],
     )(*results)
 
 

time: 43.1 us -> 38.8 us (0.900)
  the two profiles are of different devices: /device:TPU:0 before, /device:TPU:17 now
where the time goes in v2:
time: 38.8 us; the launch traced here: 38 us
  Pallas kernels  37.4 us (96%)
  between operations  0.65 us (2%)
    pallas_call x1, Pallas kernels, on_device(): pl.pallas_call(functools.partial(kernel, (groups, slots, halos, fused)),...  36.5 us
    pallas_call x1, Pallas kernels, on_device(): pl.pallas_call(hand_over, out_shape=tuple((jax.ShapeDtypeStruct(value.sha...  0.9 us

profile of v2, /device:TPU:17, one launch (start us, length us, event | category | flops | bytes accessed | tf_op | source)
XLA Modules:
  0.0 38.0 jit_solution(7597793656693800951)
XLA Ops:
  0.6 36.5 %shard_map.184 = (bf16[1,128,512]{2,1,0:T(8,128)(2,1)S(1)}, f32[1,128,512]{2,1,0:T(8,128)S(1)}, f32[192,512]{1,0:T(8,128)S(1)}) custom-call(s32[1,8,8]{2,1,0:T(8,128)} %grid_rows_hbm.1, s32[1,8]{1,0:T(1,128)} %counts_hbm.1, s32[1,4,8]{2,1,0:T(4,128)} %bitcast.7, s32[1,1024]{1,0:T(1,128)} %bitcast.5, s32[1,1024]{1,0:T(1,128)} %bitcast.6, s32[1,512]{1,0:T(1,128)} %bitcast.8, ...), custom_call_target="tpu_custom_call" | custom-call | tf_op jit(solution)/shard_map/pallas_call | solution.py:414
  37.1 0.9 %shard_map.185 = (bf16[1,128,512]{2,1,0:T(8,128)(2,1)}, f32[1,128,512]{2,1,0:T(8,128)}, f32[192,512]{1,0:T(8,128)}) custom-call(bf16[1,128,512]{2,1,0:T(8,128)(2,1)S(1)} %get-tuple-element.6.refs_0_, f32[1,128,512]{2,1,0:T(8,128)S(1)} %get-tuple-element.7.refs_1_, f32[192,512]{1,0:T(8,128)S(1)} %get-tuple-element.8.refs_2_), custom_call_target="tpu_custom_call" | custom-call | tf_op jit(solution)/shard_map/pallas_call | solution.py:445

commit v3 on v2

--- a/solution.py
+++ b/solution.py
@@ -242,7 +242,7 @@
 
     kind = BF if fused else F32
     target = grads if fused else weights_ref
-    unit = staged.shape[1]
+    unit = staged.shape[2]
     waiting = list(range(groups))
 
     def rows_of(block, side):
@@ -258,48 +258,61 @@
     def store_part(number, value):
         target[number * width : (number + 1) * width, :] = value.astype(kind)
 
-    def send_pairs(ready_from):
-        while waiting and waiting[-1] * 2 * unit >= ready_from:
-            pair_copy(waiting.pop()).start()
+    def send_pairs(first, past):
+        for block in [b for b in waiting if first <= b * 2 * unit and (b + 1) * 2 * unit <= past]:
+            waiting.remove(block)
+            pair_copy(block).start()
 
     quarter = unit // 2
     lines = groups // COLUMNS
     steps = [(1, 0), (0, 1), (1, 1)]
 
-    def plane_copy(row, k):
+    def plane_copy(row, part, k):
         dx, dy = steps[k]
         x, y = lax.rem(far + dx, 2), lax.rem(column + dy, COLUMNS)
         return pltpu.make_async_remote_copy(
-            src_ref=staged.at[COLUMNS * row + y, pl.ds(pl.multiple_of(x * quarter, TILE), quarter)],
-            dst_ref=plane_recv.at[row, k],
-            send_sem=plane_sem.at[0, row, k], recv_sem=plane_sem.at[1, row, k],
+            src_ref=staged.at[COLUMNS * row + y, part, pl.ds(pl.multiple_of(x * quarter, TILE), quarter)],
+            dst_ref=plane_recv.at[row, part, k],
+            send_sem=plane_sem.at[0, row, part, k], recv_sem=plane_sem.at[1, row, part, k],
             device_id={"graph": COLUMNS * line + y, "sample": 2 * x + half}, device_id_type=pl.DeviceIdType.MESH,
         )
 
-    def line_copy(row, slot):
+    def line_copy(row, part, slot):
         return pltpu.make_async_remote_copy(
-            src_ref=line_send.at[row], dst_ref=line_recv.at[slot],
-            send_sem=line_sem.at[0, row], recv_sem=line_sem.at[1, slot],
+            src_ref=line_send.at[row, part], dst_ref=line_recv.at[slot, part],
+            send_sem=line_sem.at[0, row, part], recv_sem=line_sem.at[1, slot, part],
             device_id={"graph": COLUMNS * row + column}, device_id_type=pl.DeviceIdType.MESH,
         )
 
-    def last_copy(k):
+    def last_copy(part, k):
         return pltpu.make_async_remote_copy(
-            src_ref=last_send, dst_ref=last_recv.at[k],
-            send_sem=last_sem.at[0, k], recv_sem=last_sem.at[1, k],
+            src_ref=last_send.at[part], dst_ref=last_recv.at[part, k],
+            send_sem=last_sem.at[0, part, k], recv_sem=last_sem.at[1, part, k],
             device_id={"sample": sample_at(*steps[k])}, device_id_type=pl.DeviceIdType.MESH,
         )
 
-    def stage_row(row):
+    parts = staged.shape[1] if fused else 1
+    lanes = width // parts
+
+    def columns_of(part):
+        return pl.ds(part * lanes, lanes)
+
+    def stage_row(row, which):
         for block in range(COLUMNS * row, COLUMNS * (row + 1)):
-            pair_copy(block).wait()
-            staged[block] = (grads[rows_of(block, half), :].astype(F32) + pair_recv[block].astype(F32)).astype(BF)
-        for k in (2, 0, 1):
-            plane_copy(row, k).start()
+            if which[0] == 0:
+                pair_copy(block).wait()
+            for part in which:
+                staged[block, part] = (
+                    grads[rows_of(block, half), columns_of(part)].astype(F32)
+                    + pair_recv[block, :, columns_of(part)].astype(F32)
+                ).astype(BF)
+        for part in which:
+            for k in (2, 0, 1):
+                plane_copy(row, part, k).start()
 
     store_part(2, inner_rows(aggregate, d_update))
     if fused:
-        send_pairs(2 * width)
+        send_pairs(2 * width, 3 * width)
     d_both = jnp.zeros((padded + 2 * mesh_rows, width), F32)
     for first in range(0, mesh_edges, chunk):
         d_pre = (inner_rows(recv_hot[:, first : first + chunk], d_aggregate) * slope_v[first : first + chunk, :]).astype(BF)
@@ -308,11 +321,15 @@
     halo_grad = d_both[:padded]
     send_grad = d_both[padded : padded + mesh_rows]
     recv_grad = d_both[padded + mesh_rows :]
+    if fused:
+        store_part(0, inner_rows(halo, halo_grad) + inner_rows(latent, send_grad))
+        send_pairs(0, width)
+        store_part(1, inner_rows(latent, recv_grad))
+        send_pairs(0, 3 * width)
+        stage_row(lines - 1, [0])
     back_send[...] = times_transposed(halo_grad, a_send_v[...]).astype(BF).reshape(groups, PAD, width)
     swap_start(2, back_send, back_recv)
     back_recv[me] = back_send[me]
-    if fused:
-        stage_row(lines - 1)
 
     def finish_mesh():
         local_grad[...] = cot + times_transposed(recv_grad, a_recv_v[...]) + times_transposed(send_grad, a_send_v[...])
@@ -325,55 +342,57 @@
         finish_mesh()
         return
 
-    store_part(1, inner_rows(latent, recv_grad))
-    send_pairs(width)
-    store_part(0, inner_rows(halo, halo_grad) + inner_rows(latent, send_grad))
-    send_pairs(0)
-    order = [lines - 1] + list(range(lines - 1))
-    for row in order[1:]:
-        stage_row(row)
+    every = list(range(parts))
+    for row in range(lines - 1):
+        stage_row(row, every)
+        if row == 0 and parts > 1:
+            stage_row(lines - 1, every[1:])
     finish_mesh()
 
     own_rows = pl.ds(pl.multiple_of(far * quarter, TILE), quarter)
 
     def finish_row():
-        total = line_send[line].astype(F32)
+        for part in every:
+            total = line_send[line, part].astype(F32)
+            for step in range(1, lines):
+                row = lax.rem(line + step, lines)
+                line_copy(row, part, row).wait_recv()
+                total = total + line_recv[row, part].astype(F32)
+            last_send[part] = total.astype(BF)
+            for k in (2, 0, 1):
+                last_copy(part, k).start()
+
+    order = [(lines - 1, 0)] + [(0, part) for part in every] + [(lines - 1, part) for part in every[1:]]
+    order += [(row, part) for row in range(1, lines - 1) for part in every]
+    for row, part in order:
+        total = staged[COLUMNS * row + column, part, own_rows, :].astype(F32)
+        for k in range(3):
+            plane_copy(row, part, k).wait()
+            total = total + plane_recv[row, part, k].astype(F32)
+        line_send[row, part] = total.astype(BF)
+
+        @pl.when(line != row)
+        def _():
+            line_copy(row, part, line).start()
+
+        if (row, part) == (lines - 2, 0):
+            pl.when(line == 0)(finish_row)
+    pl.when(line != 0)(finish_row)
+
+    def place(k, part, value):
+        dx, dc = steps[k] if k >= 0 else (0, 0)
+        start = lax.rem(half + dc, 2) * unit + lax.rem(far + dx, 2) * quarter
+        weights_ref[pl.ds(pl.multiple_of(start, TILE), quarter), columns_of(part)] = value.astype(F32)
+
+    for part in every:
+        place(-1, part, last_send[part])
         for step in range(1, lines):
             row = lax.rem(line + step, lines)
-            line_copy(row, row).wait_recv()
-            total = total + line_recv[row].astype(F32)
-        last_send[...] = total.astype(BF)
-        for k in (2, 0, 1):
-            last_copy(k).start()
-
-    for row in order:
-        total = staged[COLUMNS * row + column, own_rows, :].astype(F32)
-        for k in range(3):
-            plane_copy(row, k).wait()
-            total = total + plane_recv[row, k].astype(F32)
-        line_send[row] = total.astype(BF)
-
-        @pl.when(line != row)
-        def _():
-            line_copy(row, line).start()
-
-        if row == lines - 2:
-            pl.when(line != 0)(finish_row)
-        if row == lines - 3:
-            pl.when(line == 0)(finish_row)
-
-    def place(k, value):
-        dx, dc = steps[k] if k >= 0 else (0, 0)
-        start = lax.rem(half + dc, 2) * unit + lax.rem(far + dx, 2) * quarter
-        weights_ref[pl.ds(pl.multiple_of(start, TILE), quarter), :] = value
-
-    place(-1, last_send[...].astype(F32))
-    for step in range(1, lines):
-        row = lax.rem(line + step, lines)
-        line_copy(row, row).wait_send()
-    for k in (1, 0, 2):
-        last_copy(k).wait()
-        place(k, last_recv[k].astype(F32))
+            line_copy(row, part, row).wait_send()
+    for part in every:
+        for k in (1, 0, 2):
+            last_copy(part, k).wait()
+            place(k, part, last_recv[part, k])
 
 
 def hand_over(*refs):
@@ -403,6 +422,8 @@
     one = groups if fused else 1
     quarter = unit // 2 if fused else TILE
     lines = groups // COLUMNS if fused else 1
+    parts = 2 if width % 256 == 0 else 1
+    lanes = width // parts
     vmem = pl.BlockSpec(memory_space=pltpu.VMEM)
     hbm = pl.BlockSpec(memory_space=pltpu.HBM)
     slab = pltpu.VMEM((groups, PAD, width), BF)
@@ -425,12 +446,13 @@
             pltpu.VMEM((edges, width), F32), pltpu.VMEM((mesh_edges, width), F32),
             pltpu.VMEM((mesh_rows, width), F32),
             pltpu.VMEM((3 * width, width) if fused else (TILE, width), BF),
-            pltpu.VMEM((one, unit, width), BF), pltpu.VMEM((one, unit, width), BF),
-            pltpu.VMEM((lines, 3, quarter, width), BF), pltpu.VMEM((lines, quarter, width), BF),
-            pltpu.VMEM((lines, quarter, width), BF), pltpu.VMEM((quarter, width), BF), pltpu.VMEM((3, quarter, width), BF),
+            pltpu.VMEM((one, unit, width), BF), pltpu.VMEM((one, parts, unit, lanes), BF),
+            pltpu.VMEM((lines, parts, 3, quarter, lanes), BF), pltpu.VMEM((lines, parts, quarter, lanes), BF),
+            pltpu.VMEM((lines, parts, quarter, lanes), BF), pltpu.VMEM((parts, quarter, lanes), BF),
+            pltpu.VMEM((parts, 3, quarter, lanes), BF),
             pltpu.SemaphoreType.DMA((8,)), pltpu.SemaphoreType.DMA((9,)), pltpu.SemaphoreType.DMA((3, groups)), pltpu.SemaphoreType.DMA((3, groups)),
-            pltpu.SemaphoreType.DMA((2, groups)), pltpu.SemaphoreType.DMA((2, lines, 3)),
-            pltpu.SemaphoreType.DMA((2, lines)), pltpu.SemaphoreType.DMA((2, 3)),
+            pltpu.SemaphoreType.DMA((2, groups)), pltpu.SemaphoreType.DMA((2, lines, parts, 3)),
+            pltpu.SemaphoreType.DMA((2, lines, parts)), pltpu.SemaphoreType.DMA((2, parts, 3)),
         ],
         compiler_params=pltpu.CompilerParams(
             collective_id=0, has_side_effects=True, vmem_limit_bytes=LIMIT

time: 38.8 us -> 37.8 us (0.974)
  Pallas kernels: 37.4 us -> 36.8 us
    pallas_call x1, Pallas kernels: 36.5 us -> 35.9 us  [on_device(): pl.pallas_call(functools.partial(kernel, (groups, slots, halos, fused)),...]
where the time goes in v3:
time: 37.8 us; the launch traced here: 37.4 us
  Pallas kernels  36.8 us (97%)
  between operations  0.65 us (2%)
    pallas_call x1, Pallas kernels, on_device(): pl.pallas_call(functools.partial(kernel, (groups, slots, halos, fused)),...  35.9 us
    pallas_call x1, Pallas kernels, on_device(): pl.pallas_call(hand_over, out_shape=tuple((jax.ShapeDtypeStruct(value.sha...  0.9 us

profile of v3, /device:TPU:17, one launch (start us, length us, event | category | flops | bytes accessed | tf_op | source)
XLA Modules:
  0.0 37.4 jit_solution(2557181751849132195)
XLA Ops:
  0.6 35.9 %shard_map.184 = (bf16[1,128,512]{2,1,0:T(8,128)(2,1)S(1)}, f32[1,128,512]{2,1,0:T(8,128)S(1)}, f32[192,512]{1,0:T(8,128)S(1)}) custom-call(s32[1,8,8]{2,1,0:T(8,128)} %grid_rows_hbm.1, s32[1,8]{1,0:T(1,128)} %counts_hbm.1, s32[1,4,8]{2,1,0:T(4,128)} %bitcast.7, s32[1,1024]{1,0:T(1,128)} %bitcast.5, s32[1,1024]{1,0:T(1,128)} %bitcast.6, s32[1,512]{1,0:T(1,128)} %bitcast.8, ...), custom_call_target="tpu_custom_call" | custom-call | tf_op jit(solution)/shard_map/pallas_call | solution.py:435
  36.5 0.9 %shard_map.185 = (bf16[1,128,512]{2,1,0:T(8,128)(2,1)}, f32[1,128,512]{2,1,0:T(8,128)}, f32[192,512]{1,0:T(8,128)}) custom-call(bf16[1,128,512]{2,1,0:T(8,128)(2,1)S(1)} %get-tuple-element.6.refs_0_, f32[1,128,512]{2,1,0:T(8,128)S(1)} %get-tuple-element.7.refs_1_, f32[192,512]{1,0:T(8,128)S(1)} %get-tuple-element.8.refs_2_), custom_call_target="tpu_custom_call" | custom-call | tf_op jit(solution)/shard_map/pallas_call | solution.py:467

commit v4 on v3

--- a/solution.py
+++ b/solution.py
@@ -48,6 +48,10 @@
 def spread(table, pattern):
     low = lax.rem(table, 256)
     return dot(lax.div(table, 256).astype(BF), pattern) * 256.0 + dot(low.astype(BF), pattern)
+
+
+def wait_bytes(ref, sem):
+    pltpu.make_async_copy(ref, ref, sem).wait()
 
 
 def slot_rows(grid_rows_ref, counts_ref, halo_rows_ref, groups, padded, halos):
@@ -83,7 +87,7 @@
     grid_v, init_v, w_embed_v, w_g2m_v, a_send_v, a_recv_v, b_node_v, cot_v,
     lat_send, lat_recv, halo_send, halo_recv, back_send, back_recv,
     geo_part, slope_v, local_grad, grads, pair_recv, staged, plane_recv, line_send, line_recv, last_send, last_recv,
-    load_sem, small_sem, g_send_sem, g_recv_sem, pair_sem, plane_sem, line_sem, last_sem,
+    load_sem, small_sem, swap_sem, pair_sem, plane_sem, line_sem, last_sem,
 ):
     groups, slots, halos, fused = cfg
     me = lax.axis_index("graph")
@@ -140,27 +144,23 @@
             )
         greeted += 4
 
-    def swap_copy(kind, src, dst, peer, slot):
-        return pltpu.make_async_remote_copy(
-            src_ref=src, dst_ref=dst, send_sem=g_send_sem.at[kind, peer], recv_sem=g_recv_sem.at[kind, slot],
-            device_id={"graph": peer}, device_id_type=pl.DeviceIdType.MESH,
-        )
-
     def swap_start(kind, source, target):
         def body(step, carry):
             peer = lax.rem(me + step, groups)
-            swap_copy(kind, source.at[peer], target.at[me], peer, me).start()
+            pltpu.make_async_remote_copy(
+                src_ref=source.at[peer], dst_ref=target.at[me], send_sem=swap_sem.at[0, kind], recv_sem=swap_sem.at[1, kind],
+                device_id={"graph": peer}, device_id_type=pl.DeviceIdType.MESH,
+            ).start()
             return carry
 
         lax.fori_loop(1, groups, body, 0)
 
-    def swap_wait(kind, source, target):
-        def body(step, carry):
-            peer = lax.rem(me + step, groups)
-            swap_copy(kind, source.at[peer], target.at[peer], peer, peer).wait()
-            return carry
-
-        lax.fori_loop(1, groups, body, 0)
+    def swap_wait(kind, target):
+        wait_bytes(target.at[pl.ds(0, groups - 1)], swap_sem.at[1, kind])
+
+    def swaps_sent():
+        for kind, source in enumerate((lat_send, halo_send, back_send)):
+            wait_bytes(source.at[pl.ds(0, groups - 1)], swap_sem.at[0, kind])
 
     width = w_g2m_v.shape[1]
     mesh_rows = init_v.shape[0]
@@ -189,7 +189,7 @@
     recv_hot_g = hot(mesh_rows, g2m_receivers_ref[...])
     ld_g2m.wait()
     ld_init.wait()
-    swap_wait(0, lat_send, lat_recv)
+    swap_wait(0, lat_recv)
     grid_proj = dot(lat_recv[...].reshape(padded, width), w_g2m_v[...])
     grid_proj = two_terms(grid_proj)
     grid_hot = jnp.concatenate([grid_hot, grid_hot], axis=0)
@@ -218,7 +218,7 @@
     send_hot = hot(padded + mesh_rows, table_row)
     ld_bnode.wait()
     ld_cot.wait()
-    swap_wait(1, halo_send, halo_recv)
+    swap_wait(1, halo_recv)
     halo = halo_recv[...].reshape(padded, width)
     halo_proj = dot(halo, a_send_v[...])
     all_proj = two_terms(jnp.concatenate([halo_proj, local_proj, recv_proj], axis=0))
@@ -243,6 +243,9 @@
     kind = BF if fused else F32
     target = grads if fused else weights_ref
     unit = staged.shape[2]
+    parts = staged.shape[1]
+    lanes = width // parts
+    lines = groups // COLUMNS
     waiting = list(range(groups))
 
     def rows_of(block, side):
@@ -251,7 +254,7 @@
     def pair_copy(block):
         return pltpu.make_async_remote_copy(
             src_ref=grads.at[rows_of(block, 1 - half)], dst_ref=pair_recv.at[block],
-            send_sem=pair_sem.at[0, block], recv_sem=pair_sem.at[1, block],
+            send_sem=pair_sem.at[lines], recv_sem=pair_sem.at[block // COLUMNS],
             device_id={"sample": core_peer}, device_id_type=pl.DeviceIdType.MESH,
         )
 
@@ -264,7 +267,6 @@
             pair_copy(block).start()
 
     quarter = unit // 2
-    lines = groups // COLUMNS
     steps = [(1, 0), (0, 1), (1, 1)]
 
     def plane_copy(row, part, k):
@@ -273,34 +275,31 @@
         return pltpu.make_async_remote_copy(
             src_ref=staged.at[COLUMNS * row + y, part, pl.ds(pl.multiple_of(x * quarter, TILE), quarter)],
             dst_ref=plane_recv.at[row, part, k],
-            send_sem=plane_sem.at[0, row, part, k], recv_sem=plane_sem.at[1, row, part, k],
+            send_sem=plane_sem.at[lines, 0], recv_sem=plane_sem.at[row, part],
             device_id={"graph": COLUMNS * line + y, "sample": 2 * x + half}, device_id_type=pl.DeviceIdType.MESH,
         )
 
     def line_copy(row, part, slot):
         return pltpu.make_async_remote_copy(
             src_ref=line_send.at[row, part], dst_ref=line_recv.at[slot, part],
-            send_sem=line_sem.at[0, row, part], recv_sem=line_sem.at[1, slot, part],
+            send_sem=line_sem.at[parts], recv_sem=line_sem.at[part],
             device_id={"graph": COLUMNS * row + column}, device_id_type=pl.DeviceIdType.MESH,
         )
 
     def last_copy(part, k):
         return pltpu.make_async_remote_copy(
             src_ref=last_send.at[part], dst_ref=last_recv.at[part, k],
-            send_sem=last_sem.at[0, part, k], recv_sem=last_sem.at[1, part, k],
+            send_sem=last_sem.at[parts], recv_sem=last_sem.at[part],
             device_id={"sample": sample_at(*steps[k])}, device_id_type=pl.DeviceIdType.MESH,
         )
 
-    parts = staged.shape[1] if fused else 1
-    lanes = width // parts
-
     def columns_of(part):
         return pl.ds(part * lanes, lanes)
 
     def stage_row(row, which):
+        if which[0] == 0:
+            wait_bytes(pair_recv.at[pl.ds(COLUMNS * row, COLUMNS)], pair_sem.at[row])
         for block in range(COLUMNS * row, COLUMNS * (row + 1)):
-            if which[0] == 0:
-                pair_copy(block).wait()
             for part in which:
                 staged[block, part] = (
                     grads[rows_of(block, half), columns_of(part)].astype(F32)
@@ -333,13 +332,14 @@
 
     def finish_mesh():
         local_grad[...] = cot + times_transposed(recv_grad, a_recv_v[...]) + times_transposed(send_grad, a_send_v[...])
-        swap_wait(2, back_send, back_recv)
+        swap_wait(2, back_recv)
         grad_ref[0] = local_grad[...] + dot(pick_halo, back_recv[...].reshape(padded, width))
 
     if not fused:
         store_part(1, inner_rows(latent, recv_grad))
         store_part(0, inner_rows(halo, halo_grad) + inner_rows(latent, send_grad))
         finish_mesh()
+        swaps_sent()
         return
 
     every = list(range(parts))
@@ -354,9 +354,9 @@
     def finish_row():
         for part in every:
             total = line_send[line, part].astype(F32)
+            wait_bytes(line_recv.at[pl.ds(0, lines - 1), part], line_sem.at[part])
             for step in range(1, lines):
                 row = lax.rem(line + step, lines)
-                line_copy(row, part, row).wait_recv()
                 total = total + line_recv[row, part].astype(F32)
             last_send[part] = total.astype(BF)
             for k in (2, 0, 1):
@@ -366,8 +366,8 @@
     order += [(row, part) for row in range(1, lines - 1) for part in every]
     for row, part in order:
         total = staged[COLUMNS * row + column, part, own_rows, :].astype(F32)
+        wait_bytes(plane_recv.at[row, part], plane_sem.at[row, part])
         for k in range(3):
-            plane_copy(row, part, k).wait()
             total = total + plane_recv[row, part, k].astype(F32)
         line_send[row, part] = total.astype(BF)
 
@@ -386,13 +386,15 @@
 
     for part in every:
         place(-1, part, last_send[part])
-        for step in range(1, lines):
-            row = lax.rem(line + step, lines)
-            line_copy(row, part, row).wait_send()
+    swaps_sent()
+    wait_bytes(pair_recv, pair_sem.at[lines])
+    wait_bytes(plane_recv, plane_sem.at[lines, 0])
+    wait_bytes(line_send.at[pl.ds(0, lines - 1)], line_sem.at[parts])
     for part in every:
-        for k in (1, 0, 2):
-            last_copy(part, k).wait()
+        wait_bytes(last_recv.at[part], last_sem.at[part])
+        for k in range(3):
             place(k, part, last_recv[part, k])
+    wait_bytes(last_recv, last_sem.at[parts])
 
 
 def hand_over(*refs):
@@ -450,9 +452,9 @@
             pltpu.VMEM((lines, parts, 3, quarter, lanes), BF), pltpu.VMEM((lines, parts, quarter, lanes), BF),
             pltpu.VMEM((lines, parts, quarter, lanes), BF), pltpu.VMEM((parts, quarter, lanes), BF),
             pltpu.VMEM((parts, 3, quarter, lanes), BF),
-            pltpu.SemaphoreType.DMA((8,)), pltpu.SemaphoreType.DMA((9,)), pltpu.SemaphoreType.DMA((3, groups)), pltpu.SemaphoreType.DMA((3, groups)),
-            pltpu.SemaphoreType.DMA((2, groups)), pltpu.SemaphoreType.DMA((2, lines, parts, 3)),
-            pltpu.SemaphoreType.DMA((2, lines, parts)), pltpu.SemaphoreType.DMA((2, parts, 3)),
+            pltpu.SemaphoreType.DMA((8,)), pltpu.SemaphoreType.DMA((9,)), pltpu.SemaphoreType.DMA((2, 3)),
+            pltpu.SemaphoreType.DMA((lines + 1,)), pltpu.SemaphoreType.DMA((lines + 1, parts)),
+            pltpu.SemaphoreType.DMA((parts + 1,)), pltpu.SemaphoreType.DMA((parts + 1,)),
         ],
         compiler_params=pltpu.CompilerParams(
             collective_id=0, has_side_effects=True, vmem_limit_bytes=LIMIT

time: 37.8 us -> 36.8 us (0.974)
  Pallas kernels: 36.8 us -> 35.7 us
    pallas_call x1, Pallas kernels: 35.9 us -> 34.8 us  [on_device(): pl.pallas_call(functools.partial(kernel, (groups, slots, halos, fused)),...]
where the time goes in v4:
time: 36.8 us; the launch traced here: 36.4 us
  Pallas kernels  35.7 us (97%)
  between operations  0.65 us (2%)
    pallas_call x1, Pallas kernels, on_device(): pl.pallas_call(functools.partial(kernel, (groups, slots, halos, fused)),...  34.8 us
    pallas_call x1, Pallas kernels, on_device(): pl.pallas_call(hand_over, out_shape=tuple((jax.ShapeDtypeStruct(value.sha...  0.9 us

profile of v4, /device:TPU:17, one launch (start us, length us, event | category | flops | bytes accessed | tf_op | source)
XLA Modules:
  0.0 36.4 jit_solution(5925914146480245073)
XLA Ops:
  0.6 34.8 %shard_map.184 = (bf16[1,128,512]{2,1,0:T(8,128)(2,1)S(1)}, f32[1,128,512]{2,1,0:T(8,128)S(1)}, f32[192,512]{1,0:T(8,128)S(1)}) custom-call(s32[1,8,8]{2,1,0:T(8,128)} %grid_rows_hbm.1, s32[1,8]{1,0:T(1,128)} %counts_hbm.1, s32[1,4,8]{2,1,0:T(4,128)} %bitcast.7, s32[1,1024]{1,0:T(1,128)} %bitcast.5, s32[1,1024]{1,0:T(1,128)} %bitcast.6, s32[1,512]{1,0:T(1,128)} %bitcast.8, ...), custom_call_target="tpu_custom_call" | custom-call | tf_op jit(solution)/shard_map/pallas_call | solution.py:437
  35.5 0.9 %shard_map.185 = (bf16[1,128,512]{2,1,0:T(8,128)(2,1)}, f32[1,128,512]{2,1,0:T(8,128)}, f32[192,512]{1,0:T(8,128)}) custom-call(bf16[1,128,512]{2,1,0:T(8,128)(2,1)S(1)} %get-tuple-element.6.refs_0_, f32[1,128,512]{2,1,0:T(8,128)S(1)} %get-tuple-element.7.refs_1_, f32[192,512]{1,0:T(8,128)S(1)} %get-tuple-element.8.refs_2_), custom_call_target="tpu_custom_call" | custom-call | tf_op jit(solution)/shard_map/pallas_call | solution.py:469
